TPU v7x, 32 devices: a whole 2x2x4 slice. The times are simulated.
32 devices in a mesh: pole: 2 (over y), row: 8 (over z, x), col: 2 (over core).
Axes of the slice: x: 2, y: 2, z: 4, core: 2. Of those that a mesh axis runs over, the one named last changes fastest.
Arguments:
- known_inverse: float32 [16, 128, 1024], P('pole', 'col', 'row'), parts along dimension 0, may hold values from -1 to 3, as said below
- first_factor: float32 [2048, 512], P(('pole', 'row')), parts along dimension 0, may hold values from -0.5 to 0.5
- first_corner: float32 [1024, 512], P('pole'), parts along dimension 0, may hold values from -1 to 5, as said below
- first_ancestors: int32 [1024], P('pole'), parts along dimension 0, may hold values from 0 to 1023, as said below
- second_factor: float32 [2048, 512], P(('pole', 'row')), parts along dimension 0, may hold values from -0.75 to 0.75
- second_link: float32 [1024, 512], P('pole'), parts along dimension 0, may hold values from -0.25 to 0.25
- second_corner: float32 [1024, 512], P('pole', 'col'), parts along dimension 0, may hold values from -1 to 5, as said below
- second_ancestors: int32 [512], P('pole'), parts along dimension 0, may hold values from 0 to 1023, as said below
Outputs:
- first_column: float32 [2048, 512], P(('pole', 'row'), 'col'), parts along dimension 0
- first_diagonal: float32 [1024, 512], P('pole', 'col'), parts along dimension 0
- second_column: float32 [2048, 512], P(('pole', 'row'), 'col'), parts along dimension 0
- second_cross: float32 [1024, 512], P('pole', 'col'), parts along dimension 0
- second_diagonal: float32 [1024, 512], P('pole', 'col'), parts along dimension 0
There are 2 independent parts, one for each index of `pole`. A program takes and returns all parts, laid end to end along the dimension named above; each array names one. Nothing has to cross between parts.
Inputs may be any that keep to these rules, and one draw needn't show every extreme that they name: `known_inverse`: K is symmetric. `first_corner`: symmetric. `second_corner`: symmetric. `first_ancestors`: distinct row numbers; every block of 128 consecutive row numbers starting at a multiple of 128 holds at least one of them. `second_ancestors`: distinct row numbers, each of which is also in first_ancestors; every block of 128 consecutive row numbers starting at a multiple of 128 holds at least one of them.
All inputs are finite; a program needn't handle non-finite values.
Results may differ from a plain program's by a relative error of at most 0.000084.
Values sent between devices are 32-bit elements; how exact they have to be, the bound alone decides.
A program may use at most 128 MiB of HBM per device.

v0:
```python
import functools

import jax
import jax.numpy as jnp
from jax import lax
from jax.experimental import pallas as pl
from jax.experimental.pallas import tpu as pltpu
from jax.sharding import PartitionSpec as P

HIGH = lax.Precision.HIGHEST
MESH = pl.DeviceIdType.MESH
LANES_OF_RING = 2
VMEM_FOR_WHOLE = 40 * 2**20


def product(left, right):
    return jnp.dot(left, right, precision=HIGH, preferred_element_type=jnp.float32)


def transposed_product(left, right):
    return lax.dot_general(
        left, right, (((0,), (0,)), ((), ())), precision=HIGH, preferred_element_type=jnp.float32
    )


def local_mask(ancestors, row_start, block_rows):
    global_rows = row_start + jnp.arange(block_rows, dtype=jnp.int32)
    return jnp.any(ancestors[:, None] == global_rows[None, :], axis=0).astype(jnp.float32)[:, None]


def on_device_collectives(
    known_inverse,
    first_factor,
    first_corner,
    first_ancestors,
    second_factor,
    second_link,
    second_corner,
    second_ancestors,
):
    groups, share_rows, block_rows = known_inverse.shape
    half_width = second_corner.shape[1]
    col_index = lax.axis_index("col")
    row_start = lax.axis_index("row") * block_rows
    first_mask = local_mask(first_ancestors, row_start, block_rows)
    second_mask = local_mask(second_ancestors, row_start, block_rows)
    first_masked = first_factor * first_mask
    second_masked = second_factor * second_mask
    share_start = col_index * share_rows
    first_piece = lax.dynamic_slice_in_dim(first_masked, share_start, share_rows, 0)
    second_piece = lax.dynamic_slice_in_dim(second_masked, share_start, share_rows, 0)
    columns = known_inverse.reshape(groups * share_rows, block_rows)

    def add_piece(piece):
        return transposed_product(columns, piece)

    first_partial = add_piece(lax.all_gather(first_piece, "row", axis=0, tiled=True))
    second_partial = add_piece(lax.all_gather(second_piece, "row", axis=0, tiled=True))
    first_image = lax.psum_scatter(first_partial, "col", scatter_dimension=1, tiled=True)
    first_column = -(first_image * first_mask)
    first_full = lax.all_gather(first_column, "col", axis=1, tiled=True)
    diagonal_partial = transposed_product(first_masked, first_column)
    corner_half = lax.dynamic_slice_in_dim(first_corner, col_index * half_width, half_width, 1)
    first_diagonal = corner_half - lax.psum(diagonal_partial, "row")
    diagonal_full = lax.all_gather(first_diagonal, "col", axis=1, tiled=True)
    second_image = lax.psum_scatter(second_partial, "col", scatter_dimension=1, tiled=True)
    link_half = lax.dynamic_slice_in_dim(second_link, col_index * half_width, half_width, 1)
    second_column = -((second_image + product(first_full, link_half)) * second_mask)
    second_half = lax.dynamic_slice_in_dim(second_masked, col_index * half_width, half_width, 1)
    cross_partial = transposed_product(first_full, second_half)
    closing_partial = transposed_product(second_masked, second_column)
    cross_total, closing_total = lax.psum((cross_partial, closing_partial), "row")
    second_cross = -(cross_total + product(diagonal_full, link_half))
    second_diagonal = second_corner - closing_total - transposed_product(second_link, second_cross)
    return (first_column, first_diagonal, second_column, second_cross, second_diagonal)


def split(value):
    high = value.astype(jnp.bfloat16)
    return high, (value - high.astype(jnp.float32)).astype(jnp.bfloat16)


def dot(left, right):
    return jnp.dot(left, right, preferred_element_type=jnp.float32)


def dot3(left, right):
    (left_high, left_low), (right_high, right_low) = left, right
    return dot(left_high, right_high) + (dot(left_low, right_high) + dot(left_high, right_low))


def ring_kernel(
    n,
    known,
    factor_one,
    corner_one,
    ancestors_one,
    factor_two,
    link,
    corner_two,
    ancestors_two,
    column_one,
    diagonal_one,
    column_two,
    cross_two,
    diagonal_two,
    k_raw,
    f_raw,
    f_high,
    f_low,
    t_buf,
    own,
    link_buf,
    corner_buf,
    link_half,
    corner_half,
    corner_two_buf,
    link_split,
    half_split,
    left,
    local_sem,
    ring_send,
    ring_recv,
    pair_send,
    pair_recv,
):
    half = n // 2
    blocks = half + 1
    share = k_raw.shape[3]
    block = 2 * share
    width = link_buf.shape[0]
    hw = width // 2
    me_row = lax.axis_index("row")
    me_col = lax.axis_index("col")
    other_col = 1 - me_col

    length = n // LANES_OF_RING

    def row_at(position):
        position = lax.rem(position + n, n)
        lane = position // length
        step = position + lane * (2 * length - 1 - 2 * position)
        return step * LANES_OF_RING + lane

    lane = lax.rem(me_row, LANES_OF_RING)
    step = me_row // LANES_OF_RING
    place = step + lane * (2 * length - 1 - 2 * step)
    targets = (row_at(place + 1), row_at(place - 1))

    barrier = pltpu.get_barrier_semaphore()
    for target in targets:
        pl.semaphore_signal(barrier, inc=1, device_id={"row": target}, device_id_type=MESH)
    pl.semaphore_signal(barrier, inc=1, device_id={"col": other_col}, device_id_type=MESH)

    count = [0]

    def local(src, dst):
        copy = pltpu.make_async_copy(src, dst, local_sem.at[count[0]])
        count[0] += 1
        copy.start()
        return copy

    f_one = [local(factor_one.at[pl.ds(h * share, share)], f_raw.at[0, h, 0]) for h in range(2)]
    f_two = [local(factor_two.at[pl.ds(h * share, share)], f_raw.at[0, h, 1]) for h in range(2)]
    k_own = [local(known.at[row_at(place + i)], k_raw.at[0, me_col, i]) for i in range(blocks)]
    my_columns = pl.ds(pl.multiple_of(me_col * hw, 128), hw)
    rest = [
        local(link, link_buf),
        local(corner_one, corner_buf),
        local(link.at[:, my_columns], link_half),
        local(corner_one.at[:, my_columns], corner_half),
        local(corner_two, corner_two_buf),
    ]

    def slot(direction, t):
        return 0 if t == 0 else n - 1 if t == half else 2 * t - 1 + direction

    offsets = [0] * n
    for t in range(1, half):
        offsets[slot(0, t)], offsets[slot(1, t)] = -t, t
    offsets[n - 1] = half

    def held(at):
        return blocks if offsets[at] <= 0 else half

    def view(piece, at, which, amount):
        if piece < 2:
            return f_raw.at[at, which, piece]
        return k_raw.at[at, which, pl.ds(0, amount)]

    def pieces(direction, t):
        if t < half:
            return (0, 1, 2)
        return (0,) if direction == 0 else (1, 2)

    def ring(direction, t, piece):
        return pltpu.make_async_remote_copy(
            src_ref=view(piece, slot(direction, t - 1), me_col, held(slot(direction, t))),
            dst_ref=view(piece, slot(direction, t), me_col, held(slot(direction, t))),
            send_sem=ring_send.at[direction, t - 1, piece],
            recv_sem=ring_recv.at[direction, t - 1, piece],
            device_id={"row": targets[direction]},
            device_id_type=MESH,
        )

    def pair(at, piece, which):
        return pltpu.make_async_remote_copy(
            src_ref=view(piece, at, which, held(at)),
            dst_ref=view(piece, at, which, held(at)),
            send_sem=pair_send.at[at, piece],
            recv_sem=pair_recv.at[at, piece],
            device_id={"col": other_col},
            device_id_type=MESH,
        )

    sent = []

    def go(copy):
        copy.start()
        sent.append(copy)

    pl.semaphore_wait(barrier, 3)
    for piece, waits in ((0, f_one), (1, f_two), (2, k_own)):
        for copy in waits:
            copy.wait()
        for direction in range(2):
            go(ring(direction, 1, piece))
    go(pair(0, 2, me_col))

    for copy in rest:
        copy.wait()
    link_split[0], link_split[1] = split(link_buf[...])
    half_split[0], half_split[1] = split(link_half[...])
    corner_link = dot3(split(corner_buf[...]), (half_split[0], half_split[1]))
    cross_two[...] = -corner_link
    diagonal_one[...] = corner_half[...]
    diagonal_two[...] = corner_two_buf[...] + dot3(split(link_buf[...].T), split(corner_link))
    own[...] = jnp.zeros_like(own)

    def mask_of(ancestors, row_start):
        rows = row_start + lax.broadcasted_iota(jnp.int32, (block, ancestors.shape[1]), 0)
        same = jnp.where(rows == ancestors[...], 1.0, 0.0)
        return jnp.max(same, axis=1, keepdims=True)

    def k_block(a, b):
        i = (offsets[a] - offsets[b]) % n
        if i < half or (i == half and held(b) == blocks):
            return k_raw[b, :, i].reshape(block, block)
        return k_raw[a, :, n - i].reshape(block, block).T

    def mine(ref, start):
        return ref[:, pl.ds(pl.multiple_of(start + me_col * hw, 128), hw)]

    def mine_of(ref, rows):
        return jnp.concatenate([mine(ref.at[rows], 0), mine(ref.at[rows], width)], axis=1)

    def prepare(k):
        row_start = row_at(place + offsets[k]) * block
        first = f_raw[k, :, 0].reshape(block, width) * mask_of(ancestors_one, row_start)
        second = f_raw[k, :, 1].reshape(block, width) * mask_of(ancestors_two, row_start)
        reduced = second - dot3(split(first), (link_split[0], link_split[1]))
        rows = pl.ds(k * block, block)
        both = jnp.concatenate([first, reduced], axis=1)
        f_high[rows, :], f_low[rows, :] = split(both)
        left[k % 2, 0, :, :block], left[k % 2, 1, :, :block] = split(both.T)

    def image_of(k, slots):
        if not slots:
            return jnp.zeros((block, 2 * width), jnp.float32)
        total = None
        line_high, line_low = split(jnp.concatenate([k_block(k, j) for j in slots], axis=1))
        at, start = 0, 0
        while at < len(slots):
            upto = at
            while upto + 1 < len(slots) and slots[upto + 1] == slots[upto] + 1:
                upto += 1
            past = pl.ds(slots[at] * block, (upto + 1 - at) * block)
            columns = slice(at * block, (upto + 1) * block)
            term = dot3((line_high[:, columns], line_low[:, columns]), (f_high[past, :], f_low[past, :]))
            total = term if total is None else total + term
            at = upto + 1
        return total

    def finish(k, image):
        rows = pl.ds(k * block, block)
        my_high, my_low = mine_of(f_high, rows), mine_of(f_low, rows)
        own[...] += dot3(split(k_block(0, k)), (my_high, my_low))
        diagonal_part = dot3(split(k_block(k, k)), (my_high, my_low))
        if k == 0:
            depth = block
            right_high, right_low = split(diagonal_part)
        else:
            depth = 2 * block
            t_buf[...] = image
            left[k % 2, 0, :, block:], left[k % 2, 1, :, block:] = split(image.T)
            image_mine = jnp.concatenate([mine(t_buf, 0), mine(t_buf, width)], axis=1)
            image_high, image_low = split(image_mine + diagonal_part)
            right_high = jnp.concatenate([image_high, my_high], axis=0)
            right_low = jnp.concatenate([image_low, my_low], axis=0)
        add = dot3((left[k % 2, 0, :width, :depth], left[k % 2, 1, :width, :depth]), (right_high, right_low))
        diagonal_one[...] += add[:, :hw]
        cross_two[...] += add[:, hw:]
        diagonal_two[...] += dot3(
            (left[k % 2, 0, width:, :depth], left[k % 2, 1, width:, :depth]),
            (right_high[:, hw:], right_low[:, hw:]),
        )

    def early(k, before):
        gaps = {j: (offsets[k] - offsets[j]) % n for j in range(before)}
        return [j for j, gap in gaps.items() if gap < half or (gap == half and held(j) == blocks)]

    def take(direction, t, piece):
        ring(direction, t, piece).wait_recv()
        if piece in pieces(direction, t + 1) and t < half:
            go(ring(direction, t + 1, piece))
        go(pair(slot(direction, t), piece, me_col))

    def take_both(t, piece):
        for direction in range(2):
            if piece in pieces(direction, t):
                take(direction, t, piece)

    def paired(at, which_pieces):
        for piece in which_pieces:
            pair(at, piece, other_col).wait_recv()

    paired(0, (2,))
    prepare(0)
    finish(0, None)
    for t in range(1, half + 1):
        slots = sorted({slot(0, t), slot(1, t)})
        known = min(slots)
        take_both(t, 0)
        take_both(t, 1)
        images = {}
        for k in slots:
            paired(k, (0, 1))
            prepare(k)
            images[k] = image_of(k, early(k, known))
        take_both(t, 2)
        for k in slots:
            paired(k, (2,))
            rest_of = [j for j in range(k) if j not in early(k, known)]
            finish(k, images[k] + image_of(k, rest_of))
    first_rows = mask_of(ancestors_one, me_row * block)
    second_rows = mask_of(ancestors_two, me_row * block)
    column_one[...] = -(own[:, :hw] * first_rows)
    column_two[...] = -(own[:, hw:] * second_rows)
    for copy in sent:
        copy.wait_send()


def place_kernel(*refs):
    for source, target in zip(refs[:5], refs[5:]):
        target[...] = source[...]


def on_device_ring(
    n,
    known_inverse,
    first_factor,
    first_corner,
    first_ancestors,
    second_factor,
    second_link,
    second_corner,
    second_ancestors,
):
    groups, share, block = known_inverse.shape
    width = second_link.shape[0]
    hw = second_corner.shape[1]
    f32, bf16 = jnp.float32, jnp.bfloat16
    blocks = n // 2 + 1
    anywhere = pl.BlockSpec(memory_space=pl.ANY)
    vmem = pl.BlockSpec(memory_space=pltpu.VMEM)
    square = jax.ShapeDtypeStruct((width, hw), f32)
    column = jax.ShapeDtypeStruct((block, hw), f32)
    results = pl.pallas_call(
        functools.partial(ring_kernel, n),
        out_shape=(column, square, column, square, square),
        in_specs=[anywhere, anywhere, anywhere, vmem, anywhere, anywhere, anywhere, vmem],
        out_specs=(vmem,) * 5,
        scratch_shapes=[
            pltpu.VMEM((n, 2, blocks, share, block), f32),
            pltpu.VMEM((n, 2, 2, share, width), f32),
            pltpu.VMEM((n * block, 2 * width), bf16),
            pltpu.VMEM((n * block, 2 * width), bf16),
            pltpu.VMEM((block, 2 * width), f32),
            pltpu.VMEM((block, width), f32),
            pltpu.VMEM((width, width), f32),
            pltpu.VMEM((width, width), f32),
            pltpu.VMEM((width, hw), f32),
            pltpu.VMEM((width, hw), f32),
            pltpu.VMEM((width, hw), f32),
            pltpu.VMEM((2, width, width), bf16),
            pltpu.VMEM((2, width, hw), bf16),
            pltpu.VMEM((2, 2, 2 * width, 2 * block), bf16),
            pltpu.SemaphoreType.DMA((9 + blocks,)),
            pltpu.SemaphoreType.DMA((2, n // 2, 3)),
            pltpu.SemaphoreType.DMA((2, n // 2, 3)),
            pltpu.SemaphoreType.DMA((n, 3)),
            pltpu.SemaphoreType.DMA((n, 3)),
        ],
        compiler_params=pltpu.CompilerParams(collective_id=0, has_side_effects=True),
    )(
        known_inverse,
        first_factor,
        first_corner,
        first_ancestors.reshape(1, -1),
        second_factor,
        second_link,
        second_corner,
        second_ancestors.reshape(1, -1),
    )
    return pl.pallas_call(
        place_kernel,
        out_shape=(column, square, column, square, square),
        in_specs=[vmem] * 5,
        out_specs=(vmem,) * 5,
    )(*results)


def solution(mesh):
    def on_device(*args):
        n = mesh.shape["row"]
        groups, share, block = args[0].shape
        width = args[5].shape[0]
        held = 4 * n * block * (n * block + 4 * width)
        fits = (
            mesh.shape["col"] == 2
            and n % 4 == 0
            and groups == n
            and block == 2 * share
            and held <= VMEM_FOR_WHOLE
        )
        return on_device_ring(n, *args) if fits else on_device_collectives(*args)

    return jax.shard_map(
        on_device,
        mesh=mesh,
        in_specs=(
            P("pole", "col", "row"),
            P(("pole", "row"), None),
            P("pole", None),
            P("pole"),
            P(("pole", "row"), None),
            P("pole", None),
            P("pole", "col"),
            P("pole"),
        ),
        out_specs=(
            P(("pole", "row"), "col"),
            P("pole", "col"),
            P(("pole", "row"), "col"),
            P("pole", "col"),
            P("pole", "col"),
        ),
        check_vma=False,
    )
```

profile of v0, /device:TPU:1, one launch (start us, length us, event | category | flops | bytes accessed | tf_op | source)
XLA Modules:
  0.0 51.1 jit_solution(8493160969394692016)
XLA Ops:
  0.6 47.7 %shard_map.119 = (f32[128,256]{1,0:T(8,128)}, f32[512,256]{1,0:T(8,128)}, f32[128,256]{1,0:T(8,128)}, f32[512,256]{1,0:T(8,128)}, f32[512,256]{1,0:T(8,128)}) custom-call(f32[8,64,128]{2,1,0:T(8,128)} %known.1, f32[128,512]{1,0:T(8,128)} %factor_one.1, f32[512,512]{1,0:T(8,128)} %corner_one.1, s32[1,512]{1,0:T(1,128)} %bitcast.2, f32[128,512]{1,0:T(8,128)} %factor_two.1, ...), custom_call_target="tpu_custom_call" | custom-call | tf_op jit(solution)/shard_map/pallas_call | solution.py:378
  48.4 2.7 %shard_map.120 = (f32[128,256]{1,0:T(8,128)}, f32[512,256]{1,0:T(8,128)}, f32[128,256]{1,0:T(8,128)}, f32[512,256]{1,0:T(8,128)}, f32[512,256]{1,0:T(8,128)}) custom-call(f32[128,256]{1,0:T(8,128)} %get-tuple-element.10.refs_0_, f32[512,256]{1,0:T(8,128)} %get-tuple-element.11.refs_1_, f32[128,256]{1,0:T(8,128)} %get-tuple-element.12.refs_2_, ...), custom_call_target="tpu_custom_call" | custom-call | tf_op jit(solution)/shard_map/pallas_call | solution.py:415
where the time goes:
time: 51.3 us; the launch traced here: 51.1 us
  Pallas kernels  50.4 us (98%)
  between operations  0.64 us (1%)
    pallas_call x1, Pallas kernels, on_device_ring(): pl.pallas_call(functools.partial(ring_kernel, n), out_shape=(column, squa...  47.7 us
    pallas_call x1, Pallas kernels, on_device_ring(): pl.pallas_call(place_kernel, out_shape=(column, square, column, square, s...  2.7 us

commit v1 on v0

v1 whole, which is shorter than its diff:
```python
import functools

import jax
import jax.numpy as jnp
from jax import lax
from jax.experimental import pallas as pl
from jax.experimental.pallas import tpu as pltpu
from jax.sharding import PartitionSpec as P

HIGH = lax.Precision.HIGHEST
MESH = pl.DeviceIdType.MESH
RAILS = 2
CHUNK = 64
LEAD = 3
LAG = 4
VMEM_FOR_WHOLE = 40 * 2**20


def product(left, right):
    return jnp.dot(left, right, precision=HIGH, preferred_element_type=jnp.float32)


def transposed_product(left, right):
    return lax.dot_general(
        left, right, (((0,), (0,)), ((), ())), precision=HIGH, preferred_element_type=jnp.float32
    )


def local_mask(ancestors, row_start, block_rows):
    global_rows = row_start + jnp.arange(block_rows, dtype=jnp.int32)
    return jnp.any(ancestors[:, None] == global_rows[None, :], axis=0).astype(jnp.float32)[:, None]


def on_device_collectives(
    known_inverse,
    first_factor,
    first_corner,
    first_ancestors,
    second_factor,
    second_link,
    second_corner,
    second_ancestors,
):
    groups, share_rows, block_rows = known_inverse.shape
    half_width = second_corner.shape[1]
    col_index = lax.axis_index("col")
    row_start = lax.axis_index("row") * block_rows
    first_mask = local_mask(first_ancestors, row_start, block_rows)
    second_mask = local_mask(second_ancestors, row_start, block_rows)
    first_masked = first_factor * first_mask
    second_masked = second_factor * second_mask
    share_start = col_index * share_rows
    first_piece = lax.dynamic_slice_in_dim(first_masked, share_start, share_rows, 0)
    second_piece = lax.dynamic_slice_in_dim(second_masked, share_start, share_rows, 0)
    columns = known_inverse.reshape(groups * share_rows, block_rows)

    def add_piece(piece):
        return transposed_product(columns, piece)

    first_partial = add_piece(lax.all_gather(first_piece, "row", axis=0, tiled=True))
    second_partial = add_piece(lax.all_gather(second_piece, "row", axis=0, tiled=True))
    first_image = lax.psum_scatter(first_partial, "col", scatter_dimension=1, tiled=True)
    first_column = -(first_image * first_mask)
    first_full = lax.all_gather(first_column, "col", axis=1, tiled=True)
    diagonal_partial = transposed_product(first_masked, first_column)
    corner_half = lax.dynamic_slice_in_dim(first_corner, col_index * half_width, half_width, 1)
    first_diagonal = corner_half - lax.psum(diagonal_partial, "row")
    diagonal_full = lax.all_gather(first_diagonal, "col", axis=1, tiled=True)
    second_image = lax.psum_scatter(second_partial, "col", scatter_dimension=1, tiled=True)
    link_half = lax.dynamic_slice_in_dim(second_link, col_index * half_width, half_width, 1)
    second_column = -((second_image + product(first_full, link_half)) * second_mask)
    second_half = lax.dynamic_slice_in_dim(second_masked, col_index * half_width, half_width, 1)
    cross_partial = transposed_product(first_full, second_half)
    closing_partial = transposed_product(second_masked, second_column)
    cross_total, closing_total = lax.psum((cross_partial, closing_partial), "row")
    second_cross = -(cross_total + product(diagonal_full, link_half))
    second_diagonal = second_corner - closing_total - transposed_product(second_link, second_cross)
    return (first_column, first_diagonal, second_column, second_cross, second_diagonal)


def split(value):
    high = value.astype(jnp.bfloat16)
    return high, (value - high.astype(jnp.float32)).astype(jnp.bfloat16)


def dot(left, right):
    return jnp.dot(left, right, preferred_element_type=jnp.float32)


def dot3(left, right):
    (left_high, left_low), (right_high, right_low) = left, right
    return dot(left_high, right_high) + (dot(left_low, right_high) + dot(left_high, right_low))


def chain_kernel(
    n,
    known,
    factor_one,
    corner_one,
    ancestors_one,
    factor_two,
    link,
    corner_two,
    ancestors_two,
    column_one,
    diagonal_one,
    column_two,
    cross_two,
    diagonal_two,
    k_raw,
    stage,
    raw,
    k_part,
    k_peer,
    k_full,
    select,
    own,
    inward,
    outward,
    total,
    link_buf,
    corner_buf,
    corner_two_buf,
    link_split,
    reduced,
    both,
    both_t,
    mine_split,
    k_split,
    local_sem,
    raw_send,
    raw_recv,
    hop_send,
    hop_recv,
    side_send,
    side_recv,
    pair_send,
    pair_recv,
):
    f32, bf16 = jnp.float32, jnp.bfloat16
    levels = n // RAILS
    groups, share, block = k_raw.shape
    width = link_buf.shape[0]
    hw, quarter = width // 2, width // 4
    one, two = ancestors_one.shape[1], ancestors_two.shape[1]
    rows_all = own.shape[0]
    chunks = rows_all // CHUNK
    part = one // 4
    k_start = one + two

    me_row, me_col = lax.axis_index("row"), lax.axis_index("col")
    level, rail = me_row // RAILS, lax.rem(me_row, RAILS)
    other_rail, other_col = 1 - rail, 1 - me_col
    my_quarter = 2 * me_col + rail
    side_quarter = 2 * me_col + other_rail
    near = jnp.where(level < levels // 2, 0, 1)
    far = 1 - near
    step = 1 - 2 * near
    inner = jnp.logical_and(level > 0, level < levels - 1)
    outer = jnp.logical_not(inner)
    near_row = (level + step) * RAILS + rail
    far_row = (level - step) * RAILS + rail
    side_row = level * RAILS + other_rail

    barrier = pltpu.get_barrier_semaphore()

    def greet(**place):
        pl.semaphore_signal(barrier, inc=1, device_id=place, device_id_type=MESH)

    greet(col=other_col)
    greet(row=side_row)
    greet(row=near_row)

    @pl.when(inner)
    def _():
        greet(row=far_row)

    count = [0]

    def local(src, dst):
        copy = pltpu.make_async_copy(src, dst, local_sem.at[count[0]])
        count[0] += 1
        copy.start()
        return copy

    def lanes(which):
        return pl.ds(pl.multiple_of(which * quarter, 128), quarter)

    f_stage = [
        local(factor.at[:, lanes(side_quarter)], stage.at[i])
        for i, factor in enumerate((factor_one, factor_two))
    ]
    f_own = [
        local(factor.at[:, lanes(my_quarter)], raw.at[i, rail])
        for i, factor in enumerate((factor_one, factor_two))
    ]
    k_own = local(known, k_raw)
    rest = [local(link, link_buf), local(corner_one, corner_buf), local(corner_two, corner_two_buf)]

    def remote(src, dst, send, recv, **place):
        return pltpu.make_async_remote_copy(
            src_ref=src, dst_ref=dst, send_sem=send, recv_sem=recv, device_id=place, device_id_type=MESH
        )

    def raw_copy(i):
        src = stage.at[i] if i < 2 else k_full.at[:, lanes(side_quarter)]
        return remote(src, raw.at[i, rail], raw_send.at[i], raw_recv.at[i], row=side_row)

    def k_copy():
        return remote(k_part, k_peer, raw_send.at[3], raw_recv.at[3], col=other_col)

    def rows_of(k):
        return pl.ds(pl.multiple_of(k * CHUNK, CHUNK), CHUNK)

    def hop(direction, k, src, row):
        return remote(
            src.at[rows_of(k)],
            inward.at[direction, rows_of(k)],
            hop_send.at[direction, k],
            hop_recv.at[direction, k],
            row=row,
        )

    def side_copy(k):
        at = total.at[my_quarter, rows_of(k)]
        return remote(at, at, side_send.at[k], side_recv.at[k], row=side_row)

    def pair_copy(which, k):
        at = total.at[my_quarter if which == 0 else side_quarter, rows_of(k)]
        return remote(at, at, pair_send.at[which, k], pair_recv.at[which, k], col=other_col)

    def numbers(ancestors):
        wide = jnp.broadcast_to(ancestors[...].astype(f32), (128, ancestors.shape[1]))
        return wide.T

    def selection(column):
        lane = lax.broadcasted_iota(jnp.int32, (column.shape[0], RAILS * block), 1) + level * (RAILS * block)
        repeated = jnp.concatenate([column] * (RAILS * block // 128), axis=1)
        return jnp.where(repeated == lane.astype(f32), 1.0, 0.0).astype(bf16)

    column = numbers(ancestors_one)
    select[:one, :] = selection(column)
    select[one:, :] = selection(numbers(ancestors_two))

    for copy in f_stage:
        copy.wait()
    pl.semaphore_wait(barrier, 3 + inner.astype(jnp.int32))
    raw_copy(0).start()
    raw_copy(1).start()

    k_own.wait()
    at = (
        lax.broadcasted_iota(jnp.int32, (groups, share, one), 0) * block
        + lax.broadcasted_iota(jnp.int32, (groups, share, one), 1)
        + me_col * share
    )
    pick = jnp.where(at == ancestors_one[...].reshape(1, 1, one), 1.0, 0.0).astype(bf16)
    k_high, k_low = split(k_raw[...].reshape(groups * share, block).T)
    stacked = dot(jnp.concatenate([k_high, k_low], axis=0), pick.reshape(groups * share, one))
    k_part[...] = stacked[:block] + stacked[block:]
    k_copy().start()

    def place(i, chosen):
        high, low = split(raw[i].reshape(RAILS * block, quarter))
        wide = dot(chosen, jnp.concatenate([high, low], axis=1))
        return wide[:, :quarter] + wide[:, quarter:]

    def send_own(first, last):
        @pl.when(outer)
        def _():
            for k in range(first // CHUNK, last // CHUNK):
                hop(near, k, own, near_row).start()

    for copy in f_own:
        copy.wait()
    raw_copy(0).wait_recv()
    own[:one, :] = place(0, select[:one, :])
    send_own(0, one)
    k_copy().wait_recv()
    k_full[...] = k_part[...] + k_peer[...]
    raw[2, rail] = k_full[:, lanes(my_quarter)]
    raw_copy(2).start()
    raw_copy(1).wait_recv()
    own[one:k_start, :] = place(1, select[one:, :])
    send_own(one, k_start)

    def near_event(k):
        @pl.when(inner)
        def _():
            hop(near, k, own, near_row).wait_recv()
            outward[near, rows_of(k)] = own[rows_of(k)] + inward[near, rows_of(k)]
            hop(near, k, outward.at[near], near_row).start()

    def far_event(k):
        hop(far, k, own, far_row).wait_recv()
        passed = own[rows_of(k)] + inward[far, rows_of(k)]

        @pl.when(inner)
        def _():
            outward[far, rows_of(k)] = passed
            hop(far, k, outward.at[far], far_row).start()
            total[my_quarter, rows_of(k)] = passed + inward[near, rows_of(k)]

        @pl.when(outer)
        def _():
            total[my_quarter, rows_of(k)] = passed

        side_copy(k).start()
        pair_copy(0, k).start()

    def relay(k):
        side_copy(k).wait_recv()
        pair_copy(1, k).start()

    def events(first, last):
        def body(k, carry):
            far_event(k)

            @pl.when(k + LEAD < chunks)
            def _():
                near_event(k + LEAD)

            @pl.when(k >= LAG)
            def _():
                relay(k - LAG)

            return carry

        lax.fori_loop(first, last, body, 0)

    def relays(first, last):
        def body(k, carry):
            relay(k)
            return carry

        lax.fori_loop(first, last, body, 0)

    def paired(first, last):
        def body(k, carry):
            pair_copy(0, k).wait_recv()
            pair_copy(1, k).wait_recv()
            return carry

        lax.fori_loop(first // CHUNK, last // CHUNK, body, 0)

    def mine(ref, start):
        return ref[:, pl.ds(pl.multiple_of(start + me_col * hw, 128), hw)]

    for k in range(LEAD):
        near_event(k)
    raw_copy(2).wait_recv()
    high, low = split(raw[2].reshape(RAILS * block, quarter))
    halves = jnp.concatenate([high, low], axis=1)
    for i in range(3):
        chosen = select[pl.ds(pl.multiple_of(lax.rem(my_quarter + i, 4) * part, part), part), :]
        wide = dot(chosen, halves)
        own[k_start + i * part : k_start + (i + 1) * part, :] = wide[:, :quarter] + wide[:, quarter:]
    send_own(k_start, rows_all)

    for copy in rest:
        copy.wait()
    link_split[0], link_split[1] = split(link_buf[...])
    half_split = split(mine(link_buf, 0))
    corner_link = dot3(split(corner_buf[...]), half_split)
    cross_two[...] = -corner_link
    diagonal_one[...] = mine(corner_buf, 0)
    diagonal_two[...] = corner_two_buf[...] + dot3(split(link_buf[...].T), split(corner_link))

    ready = min(chunks, one // CHUNK + LAG + 1)
    events(0, ready)
    paired(0, one)
    first = jnp.concatenate([total[q, :one, :] for q in range(4)], axis=1)
    first_split = split(first)
    both[0, :, :width], both[1, :, :width] = first_split
    both_t[0, :width, :], both_t[1, :width, :] = split(first.T)
    events(ready, chunks)
    reduced[...] = dot3(first_split, (link_split[0], link_split[1]))
    relays(chunks - LAG, chunks)

    paired(one, k_start)
    same = jnp.concatenate([column] * (two // 128), axis=1) == ancestors_two[...].astype(f32)
    spread = jnp.where(same, 1.0, 0.0).astype(bf16)
    second_high, second_low = split(jnp.concatenate([total[q, one:k_start, :] for q in range(4)], axis=1))
    second = dot(spread, second_high) + dot(spread, second_low) - reduced[...]
    both[0, :, width:], both[1, :, width:] = split(second)
    both_t[0, width:, :], both_t[1, width:, :] = split(second.T)
    for i in range(2):
        mine_split[i] = jnp.concatenate([mine(both.at[i], 0), mine(both.at[i], width)], axis=1)

    def mask_of(ancestors):
        rows = me_row * block + lax.broadcasted_iota(jnp.int32, (block, ancestors.shape[1]), 0)
        return jnp.max(jnp.where(rows == ancestors[...], 1.0, 0.0), axis=1, keepdims=True)

    mine_both = (mine_split[0], mine_split[1])
    image = dot3(split(k_full[...]), mine_both)
    column_one[...] = -(image[:, :hw] * mask_of(ancestors_one))
    column_two[...] = -(image[:, hw:] * mask_of(ancestors_two))

    def put(row, col, value):
        at = (slice(row * part, (row + 1) * part), slice(col * part, (col + 1) * part))
        k_split[(0, *at)], k_split[(1, *at)] = split(value)

    paired(k_start, rows_all)
    for q in range(4):
        for i in range(3):
            value = total[q, k_start + i * part : k_start + (i + 1) * part, :]
            put((q + i) % 4, q, value)
            if i == 1:
                put(q, (q + 1) % 4, value.T)
    grown = split(dot3((k_split[0], k_split[1]), mine_both))
    upper = dot3((both_t[0, :width, :], both_t[1, :width, :]), grown)
    diagonal_one[...] += upper[:, :hw]
    cross_two[...] += upper[:, hw:]
    diagonal_two[...] += dot3(
        (both_t[0, width:, :], both_t[1, width:, :]), (grown[0][:, hw:], grown[1][:, hw:])
    )

    for i in range(3):
        raw_copy(i).wait_send()
    k_copy().wait_send()

    def sent(k, carry):
        hop(near, k, own, near_row).wait_send()

        @pl.when(inner)
        def _():
            hop(far, k, own, far_row).wait_send()

        side_copy(k).wait_send()
        pair_copy(0, k).wait_send()
        pair_copy(1, k).wait_send()
        return carry

    lax.fori_loop(0, chunks, sent, 0)


def place_kernel(*refs):
    for source, target in zip(refs[:5], refs[5:]):
        target[...] = source[...]


def on_device_chain(
    n,
    known_inverse,
    first_factor,
    first_corner,
    first_ancestors,
    second_factor,
    second_link,
    second_corner,
    second_ancestors,
):
    groups, share, block = known_inverse.shape
    width = second_link.shape[0]
    hw, quarter = second_corner.shape[1], width // 4
    one, two = first_ancestors.shape[0], second_ancestors.shape[0]
    rows_all = one + two + 3 * (one // 4)
    chunks = rows_all // CHUNK
    f32, bf16 = jnp.float32, jnp.bfloat16
    anywhere = pl.BlockSpec(memory_space=pl.ANY)
    vmem = pl.BlockSpec(memory_space=pltpu.VMEM)
    square = jax.ShapeDtypeStruct((width, hw), f32)
    column = jax.ShapeDtypeStruct((block, hw), f32)
    results = pl.pallas_call(
        functools.partial(chain_kernel, n),
        out_shape=(column, square, column, square, square),
        in_specs=[anywhere, anywhere, anywhere, vmem, anywhere, anywhere, anywhere, vmem],
        out_specs=(vmem,) * 5,
        scratch_shapes=[
            pltpu.VMEM((groups, share, block), f32),
            pltpu.VMEM((2, block, quarter), f32),
            pltpu.VMEM((3, RAILS, block, quarter), f32),
            pltpu.VMEM((block, one), f32),
            pltpu.VMEM((block, one), f32),
            pltpu.VMEM((block, one), f32),
            pltpu.VMEM((one + two, RAILS * block), bf16),
            pltpu.VMEM((rows_all, quarter), f32),
            pltpu.VMEM((2, rows_all, quarter), f32),
            pltpu.VMEM((2, rows_all, quarter), f32),
            pltpu.VMEM((4, rows_all, quarter), f32),
            pltpu.VMEM((width, width), f32),
            pltpu.VMEM((width, width), f32),
            pltpu.VMEM((width, hw), f32),
            pltpu.VMEM((2, width, width), bf16),
            pltpu.VMEM((one, width), f32),
            pltpu.VMEM((2, one, 2 * width), bf16),
            pltpu.VMEM((2, 2 * width, one), bf16),
            pltpu.VMEM((2, one, 2 * hw), bf16),
            pltpu.VMEM((2, one, one), bf16),
            pltpu.SemaphoreType.DMA((8,)),
            pltpu.SemaphoreType.DMA((4,)),
            pltpu.SemaphoreType.DMA((4,)),
            pltpu.SemaphoreType.DMA((2, chunks)),
            pltpu.SemaphoreType.DMA((2, chunks)),
            pltpu.SemaphoreType.DMA((chunks,)),
            pltpu.SemaphoreType.DMA((chunks,)),
            pltpu.SemaphoreType.DMA((2, chunks)),
            pltpu.SemaphoreType.DMA((2, chunks)),
        ],
        compiler_params=pltpu.CompilerParams(collective_id=0, has_side_effects=True),
    )(
        known_inverse,
        first_factor,
        first_corner,
        first_ancestors.reshape(1, -1),
        second_factor,
        second_link,
        second_corner,
        second_ancestors.reshape(1, -1),
    )
    return pl.pallas_call(
        place_kernel,
        out_shape=(column, square, column, square, square),
        in_specs=[vmem] * 5,
        out_specs=(vmem,) * 5,
    )(*results)


def solution(mesh):
    def on_device(*args):
        n = mesh.shape["row"]
        groups, share, block = args[0].shape
        width = args[5].shape[0]
        one, two = args[3].shape[0], args[7].shape[0]
        held = 4 * (one + two + 3 * (one // 4)) * (width // 4) * 9 + 16 * one * (width + one)
        fits = (
            mesh.shape["col"] == 2
            and n % (2 * RAILS) == 0
            and groups == n
            and block == 2 * share
            and block % 128 == 0
            and one == width
            and width % 512 == 0
            and two % 128 == 0
            and held <= VMEM_FOR_WHOLE
        )
        return on_device_chain(n, *args) if fits else on_device_collectives(*args)

    return jax.shard_map(
        on_device,
        mesh=mesh,
        in_specs=(
            P("pole", "col", "row"),
            P(("pole", "row"), None),
            P("pole", None),
            P("pole"),
            P(("pole", "row"), None),
            P("pole", None),
            P("pole", "col"),
            P("pole"),
        ),
        out_specs=(
            P(("pole", "row"), "col"),
            P("pole", "col"),
            P(("pole", "row"), "col"),
            P("pole", "col"),
            P("pole", "col"),
        ),
        check_vma=False,
    )
```

time: 51.3 us -> 48.4 us (0.943)
  Pallas kernels: 50.4 us -> 47.3 us
    pallas_call x2, Pallas kernels: 50.4 us -> 47.3 us  [the longest x1 44.6 us: on_device_chain(): pl.pallas_call(functools.partial(chain_kernel, n), out_shape=(column, squ...]
where the time goes in v1:
time: 48.4 us; the launch traced here: 47.9 us
  Pallas kernels  47.3 us (98%)
  between operations  0.64 us (1%)
    pallas_call x1, Pallas kernels, on_device_chain(): pl.pallas_call(functools.partial(chain_kernel, n), out_shape=(column, squ...  44.6 us
    pallas_call x1, Pallas kernels, on_device_chain(): pl.pallas_call(place_kernel, out_shape=(column, square, column, square, s...  2.7 us

profile of v1, /device:TPU:1, one launch (start us, length us, event | category | flops | bytes accessed | tf_op | source)
XLA Modules:
  0.0 47.9 jit_solution(10865370105529878307)
XLA Ops:
  0.6 44.6 %shard_map.119 = (f32[128,256]{1,0:T(8,128)}, f32[512,256]{1,0:T(8,128)}, f32[128,256]{1,0:T(8,128)}, f32[512,256]{1,0:T(8,128)}, f32[512,256]{1,0:T(8,128)}) custom-call(f32[8,64,128]{2,1,0:T(8,128)} %known.1, f32[128,512]{1,0:T(8,128)} %factor_one.1, f32[512,512]{1,0:T(8,128)} %corner_one.1, s32[1,512]{1,0:T(1,128)} %bitcast.2, f32[128,512]{1,0:T(8,128)} %factor_two.1, ...), custom_call_target="tpu_custom_call" | custom-call | tf_op jit(solution)/shard_map/pallas_call | solution.py:464
  45.2 2.7 %shard_map.120 = (f32[128,256]{1,0:T(8,128)}, f32[512,256]{1,0:T(8,128)}, f32[128,256]{1,0:T(8,128)}, f32[512,256]{1,0:T(8,128)}, f32[512,256]{1,0:T(8,128)}) custom-call(f32[128,256]{1,0:T(8,128)} %get-tuple-element.10.refs_0_, f32[512,256]{1,0:T(8,128)} %get-tuple-element.11.refs_1_, f32[128,256]{1,0:T(8,128)} %get-tuple-element.12.refs_2_, ...), custom_call_target="tpu_custom_call" | custom-call | tf_op jit(solution)/shard_map/pallas_call | solution.py:511

commit v2 on v1

--- a/solution.py
+++ b/solution.py
@@ -10,9 +10,9 @@
 HIGH = lax.Precision.HIGHEST
 MESH = pl.DeviceIdType.MESH
 RAILS = 2
-CHUNK = 64
-LEAD = 3
-LAG = 4
+LEVELS = 4
+CHUNK = 128
+LAG = 3
 VMEM_FOR_WHOLE = 40 * 2**20
 
 
@@ -92,7 +92,7 @@
     return dot(left_high, right_high) + (dot(left_low, right_high) + dot(left_high, right_low))
 
 
-def chain_kernel(
+def quad_kernel(
     n,
     known,
     factor_one,
@@ -114,7 +114,8 @@
     k_peer,
     k_full,
     select,
-    own,
+    pair,
+    quad,
     inward,
     outward,
     total,
@@ -127,7 +128,9 @@
     both_t,
     mine_split,
     k_split,
+    k_last,
     local_sem,
+    k_sem,
     raw_send,
     raw_recv,
     hop_send,
@@ -138,42 +141,46 @@
     pair_recv,
 ):
     f32, bf16 = jnp.float32, jnp.bfloat16
-    levels = n // RAILS
     groups, share, block = k_raw.shape
     width = link_buf.shape[0]
     hw, quarter = width // 2, width // 4
     one, two = ancestors_one.shape[1], ancestors_two.shape[1]
-    rows_all = own.shape[0]
+    rows_all = pair.shape[0]
     chunks = rows_all // CHUNK
     part = one // 4
     k_start = one + two
+    common = (k_start + 2 * part) // CHUNK
+    pair_rows = RAILS * block
 
     me_row, me_col = lax.axis_index("row"), lax.axis_index("col")
     level, rail = me_row // RAILS, lax.rem(me_row, RAILS)
+    parity = lax.rem(level, 2)
+    mate_level = level + 1 - 2 * parity
     other_rail, other_col = 1 - rail, 1 - me_col
     my_quarter = 2 * me_col + rail
     side_quarter = 2 * me_col + other_rail
-    near = jnp.where(level < levels // 2, 0, 1)
-    far = 1 - near
-    step = 1 - 2 * near
-    inner = jnp.logical_and(level > 0, level < levels - 1)
+    my_place = RAILS * parity + rail
+    inner = jnp.logical_and(level > 0, level < LEVELS - 1)
     outer = jnp.logical_not(inner)
-    near_row = (level + step) * RAILS + rail
-    far_row = (level - step) * RAILS + rail
+    extra = me_col == 1
     side_row = level * RAILS + other_rail
+    mate_row = mate_level * RAILS + rail
+    slant_row = mate_level * RAILS + other_rail
+    across_row = (LEVELS - 1 - level) * RAILS + rail
 
     barrier = pltpu.get_barrier_semaphore()
 
     def greet(**place):
         pl.semaphore_signal(barrier, inc=1, device_id=place, device_id_type=MESH)
 
+    greet(row=slant_row)
+    greet(row=mate_row)
+    greet(row=side_row)
     greet(col=other_col)
-    greet(row=side_row)
-    greet(row=near_row)
 
     @pl.when(inner)
     def _():
-        greet(row=far_row)
+        greet(row=across_row)
 
     count = [0]
 
@@ -186,12 +193,11 @@
     def lanes(which):
         return pl.ds(pl.multiple_of(which * quarter, 128), quarter)
 
-    f_stage = [
-        local(factor.at[:, lanes(side_quarter)], stage.at[i])
-        for i, factor in enumerate((factor_one, factor_two))
-    ]
-    f_own = [
-        local(factor.at[:, lanes(my_quarter)], raw.at[i, rail])
+    f_copies = [
+        [
+            local(factor.at[:, lanes(side_quarter)], stage.at[i]),
+            local(factor.at[:, lanes(my_quarter)], raw.at[i, my_place]),
+        ]
         for i, factor in enumerate((factor_one, factor_two))
     ]
     k_own = local(known, k_raw)
@@ -202,24 +208,43 @@
             src_ref=src, dst_ref=dst, send_sem=send, recv_sem=recv, device_id=place, device_id_type=MESH
         )
 
-    def raw_copy(i):
-        src = stage.at[i] if i < 2 else k_full.at[:, lanes(side_quarter)]
-        return remote(src, raw.at[i, rail], raw_send.at[i], raw_recv.at[i], row=side_row)
+    def raw_copy(kind, i):
+        if kind == 0:
+            src = raw.at[i, my_place]
+        else:
+            src = stage.at[i] if i < 2 else k_full.at[:, lanes(side_quarter)]
+        row = (mate_row, side_row, slant_row)[kind]
+        return remote(src, raw.at[i, my_place], raw_send.at[kind, i], raw_recv.at[kind, i], row=row)
+
+    def send_raw(i):
+        @pl.when(outer)
+        def _():
+            raw_copy(0, i).start()
+            raw_copy(2, i).start()
+
+        raw_copy(1, i).start()
+
+    def wait_raw(i):
+        raw_copy(1, i).wait_recv()
+
+        @pl.when(inner)
+        def _():
+            raw_copy(0, i).wait_recv()
+            raw_copy(2, i).wait_recv()
 
     def k_copy():
-        return remote(k_part, k_peer, raw_send.at[3], raw_recv.at[3], col=other_col)
+        return remote(k_part, k_peer, k_sem.at[0], k_sem.at[1], col=other_col)
 
     def rows_of(k):
         return pl.ds(pl.multiple_of(k * CHUNK, CHUNK), CHUNK)
 
-    def hop(direction, k, src, row):
-        return remote(
-            src.at[rows_of(k)],
-            inward.at[direction, rows_of(k)],
-            hop_send.at[direction, k],
-            hop_recv.at[direction, k],
-            row=row,
-        )
+    def cross_copy(k):
+        at = rows_of(k)
+        return remote(quad.at[at], inward.at[at], hop_send.at[0, k], hop_recv.at[k], row=across_row)
+
+    def outer_copy(k):
+        at = rows_of(k)
+        return remote(outward.at[at], inward.at[at], hop_send.at[1, k], hop_recv.at[k], row=mate_row)
 
     def side_copy(k):
         at = total.at[my_quarter, rows_of(k)]
@@ -229,24 +254,35 @@
         at = total.at[my_quarter if which == 0 else side_quarter, rows_of(k)]
         return remote(at, at, pair_send.at[which, k], pair_recv.at[which, k], col=other_col)
 
+    def held(k, act, by=extra):
+        if isinstance(k, int) and k >= common:
+
+            @pl.when(by)
+            def _():
+                act(k)
+        else:
+            act(k)
+
     def numbers(ancestors):
         wide = jnp.broadcast_to(ancestors[...].astype(f32), (128, ancestors.shape[1]))
         return wide.T
 
     def selection(column):
-        lane = lax.broadcasted_iota(jnp.int32, (column.shape[0], RAILS * block), 1) + level * (RAILS * block)
-        repeated = jnp.concatenate([column] * (RAILS * block // 128), axis=1)
+        shape = (column.shape[0], 2 * pair_rows)
+        lane = lax.broadcasted_iota(jnp.int32, shape, 1) + (level // 2) * (2 * pair_rows)
+        repeated = jnp.concatenate([column] * (2 * pair_rows // 128), axis=1)
         return jnp.where(repeated == lane.astype(f32), 1.0, 0.0).astype(bf16)
 
     column = numbers(ancestors_one)
     select[:one, :] = selection(column)
     select[one:, :] = selection(numbers(ancestors_two))
-
-    for copy in f_stage:
-        copy.wait()
-    pl.semaphore_wait(barrier, 3 + inner.astype(jnp.int32))
-    raw_copy(0).start()
-    raw_copy(1).start()
+    k_last[...] = jnp.zeros_like(k_last)
+
+    for copies in f_copies:
+        for copy in copies:
+            copy.wait()
+    pl.semaphore_wait(barrier, 4 + inner.astype(jnp.int32))
+    send_raw(0)
 
     k_own.wait()
     at = (
@@ -260,102 +296,8 @@
     k_part[...] = stacked[:block] + stacked[block:]
     k_copy().start()
 
-    def place(i, chosen):
-        high, low = split(raw[i].reshape(RAILS * block, quarter))
-        wide = dot(chosen, jnp.concatenate([high, low], axis=1))
-        return wide[:, :quarter] + wide[:, quarter:]
-
-    def send_own(first, last):
-        @pl.when(outer)
-        def _():
-            for k in range(first // CHUNK, last // CHUNK):
-                hop(near, k, own, near_row).start()
-
-    for copy in f_own:
-        copy.wait()
-    raw_copy(0).wait_recv()
-    own[:one, :] = place(0, select[:one, :])
-    send_own(0, one)
-    k_copy().wait_recv()
-    k_full[...] = k_part[...] + k_peer[...]
-    raw[2, rail] = k_full[:, lanes(my_quarter)]
-    raw_copy(2).start()
-    raw_copy(1).wait_recv()
-    own[one:k_start, :] = place(1, select[one:, :])
-    send_own(one, k_start)
-
-    def near_event(k):
-        @pl.when(inner)
-        def _():
-            hop(near, k, own, near_row).wait_recv()
-            outward[near, rows_of(k)] = own[rows_of(k)] + inward[near, rows_of(k)]
-            hop(near, k, outward.at[near], near_row).start()
-
-    def far_event(k):
-        hop(far, k, own, far_row).wait_recv()
-        passed = own[rows_of(k)] + inward[far, rows_of(k)]
-
-        @pl.when(inner)
-        def _():
-            outward[far, rows_of(k)] = passed
-            hop(far, k, outward.at[far], far_row).start()
-            total[my_quarter, rows_of(k)] = passed + inward[near, rows_of(k)]
-
-        @pl.when(outer)
-        def _():
-            total[my_quarter, rows_of(k)] = passed
-
-        side_copy(k).start()
-        pair_copy(0, k).start()
-
-    def relay(k):
-        side_copy(k).wait_recv()
-        pair_copy(1, k).start()
-
-    def events(first, last):
-        def body(k, carry):
-            far_event(k)
-
-            @pl.when(k + LEAD < chunks)
-            def _():
-                near_event(k + LEAD)
-
-            @pl.when(k >= LAG)
-            def _():
-                relay(k - LAG)
-
-            return carry
-
-        lax.fori_loop(first, last, body, 0)
-
-    def relays(first, last):
-        def body(k, carry):
-            relay(k)
-            return carry
-
-        lax.fori_loop(first, last, body, 0)
-
-    def paired(first, last):
-        def body(k, carry):
-            pair_copy(0, k).wait_recv()
-            pair_copy(1, k).wait_recv()
-            return carry
-
-        lax.fori_loop(first // CHUNK, last // CHUNK, body, 0)
-
     def mine(ref, start):
         return ref[:, pl.ds(pl.multiple_of(start + me_col * hw, 128), hw)]
-
-    for k in range(LEAD):
-        near_event(k)
-    raw_copy(2).wait_recv()
-    high, low = split(raw[2].reshape(RAILS * block, quarter))
-    halves = jnp.concatenate([high, low], axis=1)
-    for i in range(3):
-        chosen = select[pl.ds(pl.multiple_of(lax.rem(my_quarter + i, 4) * part, part), part), :]
-        wide = dot(chosen, halves)
-        own[k_start + i * part : k_start + (i + 1) * part, :] = wide[:, :quarter] + wide[:, quarter:]
-    send_own(k_start, rows_all)
 
     for copy in rest:
         copy.wait()
@@ -366,17 +308,92 @@
     diagonal_one[...] = mine(corner_buf, 0)
     diagonal_two[...] = corner_two_buf[...] + dot3(split(link_buf[...].T), split(corner_link))
 
+    def contribute(i, pieces):
+        def halves(which):
+            high, low = split(raw[i, pl.ds(which * RAILS, RAILS)].reshape(pair_rows, quarter))
+            return jnp.concatenate([high, low], axis=1)
+
+        def placed(which, value, start, size):
+            columns = pl.ds(pl.multiple_of(which * pair_rows, 128), pair_rows)
+            wide = dot(select[pl.ds(start, size), columns], value)
+            return wide[:, :quarter] + wide[:, quarter:]
+
+        value = halves(parity)
+        for to, start, size in pieces:
+            pair[to : to + size, :] = placed(parity, value, start, size)
+
+        @pl.when(inner)
+        def _():
+            value = halves(1 - parity)
+            for to, start, size in pieces:
+                quad[to : to + size, :] = pair[to : to + size, :] + placed(1 - parity, value, start, size)
+            for k in range(pieces[0][0] // CHUNK, (pieces[-1][0] + pieces[-1][2]) // CHUNK):
+                held(k, lambda k: cross_copy(k).start())
+
+    wait_raw(0)
+    send_raw(1)
+    contribute(0, [(0, 0, one)])
+    k_copy().wait_recv()
+    k_full[...] = k_part[...] + k_peer[...]
+    raw[2, my_place] = k_full[:, lanes(my_quarter)]
+    send_raw(2)
+    wait_raw(1)
+    contribute(1, [(one, one, two)])
+    wait_raw(2)
+    contribute(
+        2,
+        [
+            (k_start + i * part, pl.multiple_of(lax.rem(my_quarter + i, 4) * part, part), part)
+            for i in range(3)
+        ],
+    )
+
+    def far_event(k):
+        cross_copy(k).wait_recv()
+        at = rows_of(k)
+
+        @pl.when(inner)
+        def _():
+            outward[at] = pair[at] + inward[at]
+            total[my_quarter, at] = quad[at] + inward[at]
+            outer_copy(k).start()
+
+        @pl.when(outer)
+        def _():
+            total[my_quarter, at] = pair[at] + inward[at]
+
+        side_copy(k).start()
+        pair_copy(0, k).start()
+
+    def relay(k):
+        side_copy(k).wait_recv()
+        pair_copy(1, k).start()
+
+    def paired(first, last):
+        for k in range(first // CHUNK, last // CHUNK):
+            held(k, lambda k: (pair_copy(0, k).wait_recv(), pair_copy(1, k).wait_recv()), me_col == 0)
+
+    def event(k):
+        held(k, far_event)
+        if k >= LAG:
+            held(k - LAG, relay)
+
     ready = min(chunks, one // CHUNK + LAG + 1)
-    events(0, ready)
+    for k in range(ready):
+        event(k)
     paired(0, one)
     first = jnp.concatenate([total[q, :one, :] for q in range(4)], axis=1)
     first_split = split(first)
     both[0, :, :width], both[1, :, :width] = first_split
     both_t[0, :width, :], both_t[1, :width, :] = split(first.T)
-    events(ready, chunks)
+    for k in range(ready, chunks):
+        event(k)
     reduced[...] = dot3(first_split, (link_split[0], link_split[1]))
-    relays(chunks - LAG, chunks)
-
+
+    late = list(range(chunks - LAG, chunks))
+    third = -(-LAG // 3)
+    for k in late[:third]:
+        held(k, relay)
     paired(one, k_start)
     same = jnp.concatenate([column] * (two // 128), axis=1) == ancestors_two[...].astype(f32)
     spread = jnp.where(same, 1.0, 0.0).astype(bf16)
@@ -386,6 +403,8 @@
     both_t[0, width:, :], both_t[1, width:, :] = split(second.T)
     for i in range(2):
         mine_split[i] = jnp.concatenate([mine(both.at[i], 0), mine(both.at[i], width)], axis=1)
+    for k in late[third : 2 * third]:
+        held(k, relay)
 
     def mask_of(ancestors):
         rows = me_row * block + lax.broadcasted_iota(jnp.int32, (block, ancestors.shape[1]), 0)
@@ -395,19 +414,39 @@
     image = dot3(split(k_full[...]), mine_both)
     column_one[...] = -(image[:, :hw] * mask_of(ancestors_one))
     column_two[...] = -(image[:, hw:] * mask_of(ancestors_two))
+    for k in late[2 * third :]:
+        held(k, relay)
 
     def put(row, col, value):
         at = (slice(row * part, (row + 1) * part), slice(col * part, (col + 1) * part))
         k_split[(0, *at)], k_split[(1, *at)] = split(value)
 
-    paired(k_start, rows_all)
+    def put_last(row, value):
+        at = (row // 2, slice(row % 2 * part, (row % 2 + 1) * part), slice(row % 2 * part, (row % 2 + 1) * part))
+        k_last[(0, *at)], k_last[(1, *at)] = split(value)
+
+    paired(k_start, k_start + 2 * part)
     for q in range(4):
-        for i in range(3):
-            value = total[q, k_start + i * part : k_start + (i + 1) * part, :]
-            put((q + i) % 4, q, value)
-            if i == 1:
-                put(q, (q + 1) % 4, value.T)
-    grown = split(dot3((k_split[0], k_split[1]), mine_both))
+        put(q, q, total[q, k_start : k_start + part, :])
+        value = total[q, k_start + part : k_start + 2 * part, :]
+        put((q + 1) % 4, q, value)
+        put(q, (q + 1) % 4, value.T)
+        put(q, (q + 2) % 4, jnp.zeros((part, part), f32))
+    reduced[...] = dot3((k_split[0], k_split[1]), mine_both)
+    paired(k_start + 2 * part, rows_all)
+    for q in range(2):
+        value = total[q + 2, k_start + 2 * part :, :]
+        put_last(q, value)
+        put_last(q + 2, value.T)
+    half = one // 2
+    last = [
+        dot3(
+            (k_last[0, i], k_last[1, i]),
+            (mine_split[0, (1 - i) * half : (2 - i) * half, :], mine_split[1, (1 - i) * half : (2 - i) * half, :]),
+        )
+        for i in range(2)
+    ]
+    grown = split(reduced[...] + jnp.concatenate(last, axis=0))
     upper = dot3((both_t[0, :width, :], both_t[1, :width, :]), grown)
     diagonal_one[...] += upper[:, :hw]
     cross_two[...] += upper[:, hw:]
@@ -416,22 +455,27 @@
     )
 
     for i in range(3):
-        raw_copy(i).wait_send()
+        raw_copy(1, i).wait_send()
     k_copy().wait_send()
 
-    def sent(k, carry):
-        hop(near, k, own, near_row).wait_send()
-
+    @pl.when(outer)
+    def _():
+        for i in range(3):
+            raw_copy(0, i).wait_send()
+            raw_copy(2, i).wait_send()
+
+    def sent(k):
         @pl.when(inner)
         def _():
-            hop(far, k, own, far_row).wait_send()
+            cross_copy(k).wait_send()
+            outer_copy(k).wait_send()
 
         side_copy(k).wait_send()
         pair_copy(0, k).wait_send()
         pair_copy(1, k).wait_send()
-        return carry
-
-    lax.fori_loop(0, chunks, sent, 0)
+
+    for k in range(chunks):
+        held(k, sent)
 
 
 def place_kernel(*refs):
@@ -439,7 +483,7 @@
         target[...] = source[...]
 
 
-def on_device_chain(
+def on_device_quad(
     n,
     known_inverse,
     first_factor,
@@ -462,21 +506,22 @@
     square = jax.ShapeDtypeStruct((width, hw), f32)
     column = jax.ShapeDtypeStruct((block, hw), f32)
     results = pl.pallas_call(
-        functools.partial(chain_kernel, n),
-        out_shape=(column, square, column, square, square),
+        functools.partial(quad_kernel, n),
+        out_shape=tuple(pltpu.VMEM(x.shape, x.dtype) for x in (column, square, column, square, square)),
         in_specs=[anywhere, anywhere, anywhere, vmem, anywhere, anywhere, anywhere, vmem],
         out_specs=(vmem,) * 5,
         scratch_shapes=[
             pltpu.VMEM((groups, share, block), f32),
             pltpu.VMEM((2, block, quarter), f32),
-            pltpu.VMEM((3, RAILS, block, quarter), f32),
+            pltpu.VMEM((3, 2 * RAILS, block, quarter), f32),
             pltpu.VMEM((block, one), f32),
             pltpu.VMEM((block, one), f32),
             pltpu.VMEM((block, one), f32),
-            pltpu.VMEM((one + two, RAILS * block), bf16),
+            pltpu.VMEM((one + two, 2 * RAILS * block), bf16),
             pltpu.VMEM((rows_all, quarter), f32),
-            pltpu.VMEM((2, rows_all, quarter), f32),
-            pltpu.VMEM((2, rows_all, quarter), f32),
+            pltpu.VMEM((rows_all, quarter), f32),
+            pltpu.VMEM((rows_all, quarter), f32),
+            pltpu.VMEM((rows_all, quarter), f32),
             pltpu.VMEM((4, rows_all, quarter), f32),
             pltpu.VMEM((width, width), f32),
             pltpu.VMEM((width, width), f32),
@@ -487,11 +532,13 @@
             pltpu.VMEM((2, 2 * width, one), bf16),
             pltpu.VMEM((2, one, 2 * hw), bf16),
             pltpu.VMEM((2, one, one), bf16),
+            pltpu.VMEM((2, 2, one // 2, one // 2), bf16),
             pltpu.SemaphoreType.DMA((8,)),
-            pltpu.SemaphoreType.DMA((4,)),
-            pltpu.SemaphoreType.DMA((4,)),
+            pltpu.SemaphoreType.DMA((2,)),
+            pltpu.SemaphoreType.DMA((3, 3)),
+            pltpu.SemaphoreType.DMA((3, 3)),
             pltpu.SemaphoreType.DMA((2, chunks)),
-            pltpu.SemaphoreType.DMA((2, chunks)),
+            pltpu.SemaphoreType.DMA((chunks,)),
             pltpu.SemaphoreType.DMA((chunks,)),
             pltpu.SemaphoreType.DMA((chunks,)),
             pltpu.SemaphoreType.DMA((2, chunks)),
@@ -508,6 +555,7 @@
         second_corner,
         second_ancestors.reshape(1, -1),
     )
+    results = [pltpu.with_memory_space_constraint(x, pltpu.VMEM) for x in results]
     return pl.pallas_call(
         place_kernel,
         out_shape=(column, square, column, square, square),
@@ -525,7 +573,7 @@
         held = 4 * (one + two + 3 * (one // 4)) * (width // 4) * 9 + 16 * one * (width + one)
         fits = (
             mesh.shape["col"] == 2
-            and n % (2 * RAILS) == 0
+            and n == LEVELS * RAILS
             and groups == n
             and block == 2 * share
             and block % 128 == 0
@@ -534,7 +582,7 @@
             and two % 128 == 0
             and held <= VMEM_FOR_WHOLE
         )
-        return on_device_chain(n, *args) if fits else on_device_collectives(*args)
+        return on_device_quad(n, *args) if fits else on_device_collectives(*args)
 
     return jax.shard_map(
         on_device,

time: 48.4 us -> 38.8 us (0.80)
  Pallas kernels: 47.3 us -> 38 us
    pallas_call x2, Pallas kernels: 47.3 us -> 38 us  [the longest x1 36.6 us: on_device_quad(): pl.pallas_call(functools.partial(quad_kernel, n), out_shape=tuple((pltpu....]
where the time goes in v2:
time: 38.8 us; the launch traced here: 38.6 us
  Pallas kernels  38 us (98%)
  between operations  0.64 us (2%)
    pallas_call x1, Pallas kernels, on_device_quad(): pl.pallas_call(functools.partial(quad_kernel, n), out_shape=tuple((pltpu....  36.6 us
    pallas_call x1, Pallas kernels, on_device_quad(): pl.pallas_call(place_kernel, out_shape=(column, square, column, square, s...  1.35 us

profile of v2, /device:TPU:1, one launch (start us, length us, event | category | flops | bytes accessed | tf_op | source)
XLA Modules:
  0.0 38.6 jit_solution(3629922113479264850)
XLA Ops:
  0.6 36.6 %shard_map.119 = (f32[128,256]{1,0:T(8,128)S(1)}, f32[512,256]{1,0:T(8,128)S(1)}, f32[128,256]{1,0:T(8,128)S(1)}, f32[512,256]{1,0:T(8,128)S(1)}, f32[512,256]{1,0:T(8,128)S(1)}) custom-call(f32[8,64,128]{2,1,0:T(8,128)} %known.1, f32[128,512]{1,0:T(8,128)} %factor_one.1, f32[512,512]{1,0:T(8,128)} %corner_one.1, s32[1,512]{1,0:T(1,128)} %bitcast.2, ...), custom_call_target="tpu_custom_call" | custom-call | tf_op jit(solution)/shard_map/pallas_call | solution.py:508
  37.3 1.3 %shard_map.120 = (f32[128,256]{1,0:T(8,128)}, f32[512,256]{1,0:T(8,128)}, f32[128,256]{1,0:T(8,128)}, f32[512,256]{1,0:T(8,128)}, f32[512,256]{1,0:T(8,128)}) custom-call(f32[128,256]{1,0:T(8,128)S(1)} %get-tuple-element.10.refs_0_, f32[512,256]{1,0:T(8,128)S(1)} %get-tuple-element.11.refs_1_, f32[128,256]{1,0:T(8,128)S(1)} %get-tuple-element.12.refs_2_, ...), custom_call_target="tpu_custom_call" | custom-call | tf_op jit(solution)/shard_map/pallas_call | solution.py:559

commit v3 on v2

--- a/solution.py
+++ b/solution.py
@@ -13,7 +13,10 @@
 LEVELS = 4
 CHUNK = 128
 LAG = 3
-VMEM_FOR_WHOLE = 40 * 2**20
+RAW_TWO = (0, 0)
+RAW_K = (2, 2)
+VMEM_FOR_WHOLE = 20 * 2**20
+GRANT = 57 * 2**20
 
 
 def product(left, right):
@@ -102,18 +105,21 @@
     link,
     corner_two,
     ancestors_two,
-    column_one,
     diagonal_one,
-    column_two,
     cross_two,
     diagonal_two,
+    k_full,
+    mine_split,
+    both_t,
+    grown,
+    masks,
     k_raw,
     stage,
     raw,
     k_part,
     k_peer,
-    k_full,
     select,
+    spread,
     pair,
     quad,
     inward,
@@ -125,10 +131,7 @@
     link_split,
     reduced,
     both,
-    both_t,
-    mine_split,
     k_split,
-    k_last,
     local_sem,
     k_sem,
     raw_send,
@@ -224,14 +227,6 @@
 
         raw_copy(1, i).start()
 
-    def wait_raw(i):
-        raw_copy(1, i).wait_recv()
-
-        @pl.when(inner)
-        def _():
-            raw_copy(0, i).wait_recv()
-            raw_copy(2, i).wait_recv()
-
     def k_copy():
         return remote(k_part, k_peer, k_sem.at[0], k_sem.at[1], col=other_col)
 
@@ -254,10 +249,10 @@
         at = total.at[my_quarter if which == 0 else side_quarter, rows_of(k)]
         return remote(at, at, pair_send.at[which, k], pair_recv.at[which, k], col=other_col)
 
-    def held(k, act, by=extra):
-        if isinstance(k, int) and k >= common:
-
-            @pl.when(by)
+    def held(k, act):
+        if k >= common:
+
+            @pl.when(extra)
             def _():
                 act(k)
         else:
@@ -276,7 +271,9 @@
     column = numbers(ancestors_one)
     select[:one, :] = selection(column)
     select[one:, :] = selection(numbers(ancestors_two))
-    k_last[...] = jnp.zeros_like(k_last)
+    k_split[...] = jnp.zeros_like(k_split)
+    same = jnp.concatenate([column] * (two // 128), axis=1) == ancestors_two[...].astype(f32)
+    spread[...] = jnp.where(same, 1.0, 0.0).astype(bf16)
 
     for copies in f_copies:
         for copy in copies:
@@ -308,46 +305,72 @@
     diagonal_one[...] = mine(corner_buf, 0)
     diagonal_two[...] = corner_two_buf[...] + dot3(split(link_buf[...].T), split(corner_link))
 
-    def contribute(i, pieces):
-        def halves(which):
-            high, low = split(raw[i, pl.ds(which * RAILS, RAILS)].reshape(pair_rows, quarter))
-            return jnp.concatenate([high, low], axis=1)
-
-        def placed(which, value, start, size):
-            columns = pl.ds(pl.multiple_of(which * pair_rows, 128), pair_rows)
-            wide = dot(select[pl.ds(start, size), columns], value)
-            return wide[:, :quarter] + wide[:, quarter:]
-
-        value = halves(parity)
-        for to, start, size in pieces:
-            pair[to : to + size, :] = placed(parity, value, start, size)
-
-        @pl.when(inner)
-        def _():
-            value = halves(1 - parity)
-            for to, start, size in pieces:
-                quad[to : to + size, :] = pair[to : to + size, :] + placed(1 - parity, value, start, size)
-            for k in range(pieces[0][0] // CHUNK, (pieces[-1][0] + pieces[-1][2]) // CHUNK):
-                held(k, lambda k: cross_copy(k).start())
-
-    wait_raw(0)
-    send_raw(1)
-    contribute(0, [(0, 0, one)])
-    k_copy().wait_recv()
-    k_full[...] = k_part[...] + k_peer[...]
-    raw[2, my_place] = k_full[:, lanes(my_quarter)]
-    send_raw(2)
-    wait_raw(1)
-    contribute(1, [(one, one, two)])
-    wait_raw(2)
-    contribute(
-        2,
+    def mask_of(ancestors):
+        rows = me_row * block + lax.broadcasted_iota(jnp.int32, (block, ancestors.shape[1]), 0)
+        found = jnp.max(jnp.where(rows == ancestors[...], 1.0, 0.0), axis=1, keepdims=True)
+        return jnp.broadcast_to(found, (block, 128))
+
+    masks[0], masks[1] = mask_of(ancestors_one), mask_of(ancestors_two)
+
+    def halves(i, which):
+        high, low = split(raw[i, pl.ds(which * RAILS, RAILS)].reshape(pair_rows, quarter))
+        return jnp.concatenate([high, low], axis=1)
+
+    def placed(which, value, start, size):
+        columns = pl.ds(pl.multiple_of(which * pair_rows, 128), pair_rows)
+        wide = dot(select[pl.ds(start, size), columns], value)
+        return wide[:, :quarter] + wide[:, quarter:]
+
+    pieces = (
+        [(0, 0, one)],
+        [(one, one, two)],
         [
             (k_start + i * part, pl.multiple_of(lax.rem(my_quarter + i, 4) * part, part), part)
             for i in range(3)
         ],
     )
 
+    def add_pair(i):
+        value = halves(i, parity)
+        for to, start, size in pieces[i]:
+            pair[to : to + size, :] = placed(parity, value, start, size)
+
+    def add_quad(i):
+        value = halves(i, 1 - parity)
+        for to, start, size in pieces[i]:
+            quad[to : to + size, :] = pair[to : to + size, :] + placed(1 - parity, value, start, size)
+        for k in range(pieces[i][0][0] // CHUNK, (pieces[i][-1][0] + pieces[i][-1][2]) // CHUNK):
+            held(k, lambda k: cross_copy(k).start())
+
+    raw_copy(1, 0).wait_recv()
+    add_pair(0)
+
+    @pl.when(inner)
+    def _():
+        raw_copy(0, 0).wait_recv()
+        raw_copy(2, 0).wait_recv()
+        add_quad(0)
+
+    send_raw(1)
+    k_copy().wait_recv()
+    k_full[...] = k_part[...] + k_peer[...]
+    raw[2, my_place] = k_full[:, lanes(my_quarter)]
+    send_raw(2)
+
+    @pl.when(outer)
+    def _():
+        for i in (1, 2):
+            raw_copy(1, i).wait_recv()
+            add_pair(i)
+
+    def inner_adds(i):
+        @pl.when(inner)
+        def _():
+            for kind in range(3):
+                raw_copy(kind, i).wait_recv()
+            add_pair(i)
+            add_quad(i)
+
     def far_event(k):
         cross_copy(k).wait_recv()
         at = rows_of(k)
@@ -369,90 +392,131 @@
         side_copy(k).wait_recv()
         pair_copy(1, k).start()
 
-    def paired(first, last):
+    def from_pair(first, last):
         for k in range(first // CHUNK, last // CHUNK):
-            held(k, lambda k: (pair_copy(0, k).wait_recv(), pair_copy(1, k).wait_recv()), me_col == 0)
-
-    def event(k):
-        held(k, far_event)
-        if k >= LAG:
-            held(k - LAG, relay)
-
-    ready = min(chunks, one // CHUNK + LAG + 1)
-    for k in range(ready):
-        event(k)
-    paired(0, one)
-    first = jnp.concatenate([total[q, :one, :] for q in range(4)], axis=1)
-    first_split = split(first)
-    both[0, :, :width], both[1, :, :width] = first_split
-    both_t[0, :width, :], both_t[1, :width, :] = split(first.T)
-    for k in range(ready, chunks):
-        event(k)
-    reduced[...] = dot3(first_split, (link_split[0], link_split[1]))
-
-    late = list(range(chunks - LAG, chunks))
-    third = -(-LAG // 3)
-    for k in late[:third]:
-        held(k, relay)
-    paired(one, k_start)
-    same = jnp.concatenate([column] * (two // 128), axis=1) == ancestors_two[...].astype(f32)
-    spread = jnp.where(same, 1.0, 0.0).astype(bf16)
-    second_high, second_low = split(jnp.concatenate([total[q, one:k_start, :] for q in range(4)], axis=1))
-    second = dot(spread, second_high) + dot(spread, second_low) - reduced[...]
-    both[0, :, width:], both[1, :, width:] = split(second)
-    both_t[0, width:, :], both_t[1, width:, :] = split(second.T)
-    for i in range(2):
-        mine_split[i] = jnp.concatenate([mine(both.at[i], 0), mine(both.at[i], width)], axis=1)
-    for k in late[third : 2 * third]:
-        held(k, relay)
-
-    def mask_of(ancestors):
-        rows = me_row * block + lax.broadcasted_iota(jnp.int32, (block, ancestors.shape[1]), 0)
-        return jnp.max(jnp.where(rows == ancestors[...], 1.0, 0.0), axis=1, keepdims=True)
-
-    mine_both = (mine_split[0], mine_split[1])
-    image = dot3(split(k_full[...]), mine_both)
-    column_one[...] = -(image[:, :hw] * mask_of(ancestors_one))
-    column_two[...] = -(image[:, hw:] * mask_of(ancestors_two))
-    for k in late[2 * third :]:
-        held(k, relay)
+            pair_copy(0, k).wait_recv()
+            pair_copy(1, k).wait_recv()
+
+    def keep(col, start, value, mine_too):
+        cols, at = slice(col * hw, (col + 1) * hw), slice(start + col * hw, start + (col + 1) * hw)
+        high, low = split(value)
+        both_t[0, at, :], both_t[1, at, :] = split(value.T)
+        if start == 0:
+            both[0, :, cols], both[1, :, cols] = high, low
+        if mine_too:
+            to = slice(0, hw) if start == 0 else slice(hw, 2 * hw)
+            mine_split[0, :, to], mine_split[1, :, to] = high, low
+
+    def brought(col, rows):
+        return jnp.concatenate([total[2 * col, rows, :], total[2 * col + 1, rows, :]], axis=1)
+
+    def first_half(col, add, mine_too):
+        keep(col, 0, brought(col, slice(0, one)), mine_too)
+        cols = slice(col * hw, (col + 1) * hw)
+        term = dot3((both[0, :, cols], both[1, :, cols]), (link_split[0, cols, :], link_split[1, cols, :]))
+        reduced[...] = reduced[...] + term if add else term
+
+    def second_half(col, mine_too):
+        high, low = split(brought(col, slice(one, k_start)))
+        value = dot(spread[...], high) + dot(spread[...], low) - reduced[:, col * hw : (col + 1) * hw]
+        keep(col, width, value, mine_too)
 
     def put(row, col, value):
         at = (slice(row * part, (row + 1) * part), slice(col * part, (col + 1) * part))
         k_split[(0, *at)], k_split[(1, *at)] = split(value)
 
-    def put_last(row, value):
-        at = (row // 2, slice(row % 2 * part, (row % 2 + 1) * part), slice(row % 2 * part, (row % 2 + 1) * part))
-        k_last[(0, *at)], k_last[(1, *at)] = split(value)
-
-    paired(k_start, k_start + 2 * part)
-    for q in range(4):
-        put(q, q, total[q, k_start : k_start + part, :])
-        value = total[q, k_start + part : k_start + 2 * part, :]
-        put((q + 1) % 4, q, value)
-        put(q, (q + 1) % 4, value.T)
-        put(q, (q + 2) % 4, jnp.zeros((part, part), f32))
-    reduced[...] = dot3((k_split[0], k_split[1]), mine_both)
-    paired(k_start + 2 * part, rows_all)
-    for q in range(2):
-        value = total[q + 2, k_start + 2 * part :, :]
-        put_last(q, value)
-        put_last(q + 2, value.T)
-    half = one // 2
-    last = [
-        dot3(
-            (k_last[0, i], k_last[1, i]),
-            (mine_split[0, (1 - i) * half : (2 - i) * half, :], mine_split[1, (1 - i) * half : (2 - i) * half, :]),
-        )
-        for i in range(2)
-    ]
-    grown = split(reduced[...] + jnp.concatenate(last, axis=0))
-    upper = dot3((both_t[0, :width, :], both_t[1, :width, :]), grown)
-    diagonal_one[...] += upper[:, :hw]
-    cross_two[...] += upper[:, hw:]
-    diagonal_two[...] += dot3(
-        (both_t[0, width:, :], both_t[1, width:, :]), (grown[0][:, hw:], grown[1][:, hw:])
-    )
+    def block_of(q, i):
+        return total[q, k_start + i * part : k_start + (i + 1) * part, :]
+
+    def put_diagonal(col):
+        for q in (2 * col, 2 * col + 1):
+            put(q, q, block_of(q, 0))
+
+    def put_others():
+        for q in (2, 3):
+            for i in (1, 2):
+                value = block_of(q, i)
+                put((q + i) % 4, q, value)
+                put(q, (q + i) % 4, value.T)
+
+    def grow(half):
+        rows = slice(half * (one // 2), (half + 1) * (one // 2))
+        reduced[rows, :] = dot3((k_split[0, rows], k_split[1, rows]), (mine_split[0], mine_split[1]))
+
+    def plan(col):
+        mine_chunks = common if col == 0 else chunks
+        ahead, before = one // CHUNK, k_start // CHUNK
+        for k in range(mine_chunks):
+            far_event(k)
+            if k == RAW_TWO[col]:
+                inner_adds(1)
+            if k == RAW_K[col]:
+                inner_adds(2)
+            if col == 0 and k == ahead:
+                from_pair(0, one)
+                first_half(1, False, False)
+            if col == 0 and k == min(ahead + LAG, mine_chunks - 1):
+                first_half(0, True, True)
+            if k >= LAG:
+                relay(k - LAG)
+            if col == 1 and k == ahead + LAG - 1:
+                first_half(1, False, True)
+        left = list(range(mine_chunks - LAG, mine_chunks))
+        if col == 0:
+            from_pair(one, k_start)
+            second_half(1, False)
+            for k in left:
+                if k < before:
+                    relay(k)
+            second_half(0, True)
+            later = [k for k in left if k >= before]
+            for k in later[: (len(later) + 1) // 2]:
+                relay(k)
+            from_pair(k_start, rows_all)
+            put_diagonal(1)
+            put_others()
+            put_diagonal(0)
+            grow(0)
+            for k in later[(len(later) + 1) // 2 :]:
+                relay(k)
+            grow(1)
+        else:
+            for k in left:
+                if k < common:
+                    relay(k)
+            from_pair(0, one)
+            first_half(0, True, False)
+            second_half(1, True)
+            for k in left:
+                if k >= common:
+                    relay(k)
+            put_diagonal(1)
+            put_others()
+            from_pair(one, k_start)
+            second_half(0, False)
+            from_pair(k_start, k_start + part)
+            put_diagonal(0)
+            grow(0)
+            grow(1)
+            from_pair(k_start + part, k_start + 2 * part)
+
+    for col in range(2):
+        pl.when(me_col == col)(functools.partial(plan, col))
+
+    def rows_at(q):
+        return slice(q * part, (q + 1) * part)
+
+    def mine_at(q):
+        return mine_split[0, rows_at(q)], mine_split[1, rows_at(q)]
+
+    lower = split(jnp.concatenate([block_of(0, 1).T, block_of(1, 1)], axis=0))
+    middle = split(jnp.concatenate([block_of(0, 1), block_of(1, 1).T], axis=1))
+    ends = tuple(jnp.concatenate(both_ends, axis=0) for both_ends in zip(mine_at(0), mine_at(2)))
+    outer_term = dot3(lower, mine_at(1))
+    middle_term = dot3(middle, ends)
+    for q, term in ((3, None), (0, outer_term[:part]), (2, outer_term[part:]), (1, middle_term)):
+        value = reduced[rows_at(q), :] if term is None else reduced[rows_at(q), :] + term
+        grown[0, rows_at(q)], grown[1, rows_at(q)] = split(value)
 
     for i in range(3):
         raw_copy(1, i).wait_send()
@@ -478,9 +542,45 @@
         held(k, sent)
 
 
-def place_kernel(*refs):
-    for source, target in zip(refs[:5], refs[5:]):
-        target[...] = source[...]
+def closing_kernel(
+    diagonal_one,
+    cross_two,
+    diagonal_two,
+    k_full,
+    mine_split,
+    both_t,
+    grown,
+    masks,
+    column_one_out,
+    diagonal_one_out,
+    column_two_out,
+    cross_two_out,
+    diagonal_two_out,
+    squares,
+    columns,
+    sem,
+):
+    width = diagonal_one.shape[0]
+    hw = diagonal_one.shape[1]
+    copies = []
+
+    def out(src, dst):
+        copy = pltpu.make_async_copy(src, dst, sem.at[len(copies)])
+        copy.start()
+        copies.append(copy)
+
+    sums = ((diagonal_one, 0, 0, diagonal_one_out), (cross_two, 0, hw, cross_two_out), (diagonal_two, width, hw, diagonal_two_out))
+    for i, (base, row, col, target) in enumerate(sums):
+        rows, cols = slice(row, row + width), slice(col, col + hw)
+        squares[i] = base[...] + dot3((both_t[0, rows], both_t[1, rows]), (grown[0, :, cols], grown[1, :, cols]))
+        out(squares.at[i], target)
+    image = dot3(split(k_full[...]), (mine_split[0], mine_split[1]))
+    for i, target in enumerate((column_one_out, column_two_out)):
+        mask = jnp.concatenate([masks[i]] * (hw // 128), axis=1)
+        columns[i] = -(image[:, i * hw : (i + 1) * hw] * mask)
+        out(columns.at[i], target)
+    for copy in copies:
+        copy.wait()
 
 
 def on_device_quad(
@@ -501,23 +601,33 @@
     rows_all = one + two + 3 * (one // 4)
     chunks = rows_all // CHUNK
     f32, bf16 = jnp.float32, jnp.bfloat16
-    anywhere = pl.BlockSpec(memory_space=pl.ANY)
+    anywhere = pl.BlockSpec(memory_space=pltpu.HBM)
     vmem = pl.BlockSpec(memory_space=pltpu.VMEM)
     square = jax.ShapeDtypeStruct((width, hw), f32)
     column = jax.ShapeDtypeStruct((block, hw), f32)
+    passed = (
+        square,
+        square,
+        square,
+        jax.ShapeDtypeStruct((block, one), f32),
+        jax.ShapeDtypeStruct((2, one, 2 * hw), bf16),
+        jax.ShapeDtypeStruct((2, 2 * width, one), bf16),
+        jax.ShapeDtypeStruct((2, one, 2 * hw), bf16),
+        jax.ShapeDtypeStruct((2, block, 128), f32),
+    )
     results = pl.pallas_call(
         functools.partial(quad_kernel, n),
-        out_shape=tuple(pltpu.VMEM(x.shape, x.dtype) for x in (column, square, column, square, square)),
+        out_shape=tuple(pltpu.VMEM(x.shape, x.dtype) for x in passed),
         in_specs=[anywhere, anywhere, anywhere, vmem, anywhere, anywhere, anywhere, vmem],
-        out_specs=(vmem,) * 5,
+        out_specs=(vmem,) * len(passed),
         scratch_shapes=[
             pltpu.VMEM((groups, share, block), f32),
             pltpu.VMEM((2, block, quarter), f32),
             pltpu.VMEM((3, 2 * RAILS, block, quarter), f32),
             pltpu.VMEM((block, one), f32),
             pltpu.VMEM((block, one), f32),
-            pltpu.VMEM((block, one), f32),
             pltpu.VMEM((one + two, 2 * RAILS * block), bf16),
+            pltpu.VMEM((one, two), bf16),
             pltpu.VMEM((rows_all, quarter), f32),
             pltpu.VMEM((rows_all, quarter), f32),
             pltpu.VMEM((rows_all, quarter), f32),
@@ -528,11 +638,8 @@
             pltpu.VMEM((width, hw), f32),
             pltpu.VMEM((2, width, width), bf16),
             pltpu.VMEM((one, width), f32),
-            pltpu.VMEM((2, one, 2 * width), bf16),
-            pltpu.VMEM((2, 2 * width, one), bf16),
-            pltpu.VMEM((2, one, 2 * hw), bf16),
+            pltpu.VMEM((2, one, width), bf16),
             pltpu.VMEM((2, one, one), bf16),
-            pltpu.VMEM((2, 2, one // 2, one // 2), bf16),
             pltpu.SemaphoreType.DMA((8,)),
             pltpu.SemaphoreType.DMA((2,)),
             pltpu.SemaphoreType.DMA((3, 3)),
@@ -544,7 +651,9 @@
             pltpu.SemaphoreType.DMA((2, chunks)),
             pltpu.SemaphoreType.DMA((2, chunks)),
         ],
-        compiler_params=pltpu.CompilerParams(collective_id=0, has_side_effects=True),
+        compiler_params=pltpu.CompilerParams(
+            collective_id=0, has_side_effects=True, vmem_limit_bytes=GRANT
+        ),
     )(
         known_inverse,
         first_factor,
@@ -557,10 +666,16 @@
     )
     results = [pltpu.with_memory_space_constraint(x, pltpu.VMEM) for x in results]
     return pl.pallas_call(
-        place_kernel,
+        closing_kernel,
         out_shape=(column, square, column, square, square),
-        in_specs=[vmem] * 5,
-        out_specs=(vmem,) * 5,
+        in_specs=[vmem] * len(passed),
+        out_specs=(anywhere,) * 5,
+        scratch_shapes=[
+            pltpu.VMEM((3, width, hw), f32),
+            pltpu.VMEM((2, block, hw), f32),
+            pltpu.SemaphoreType.DMA((5,)),
+        ],
+        compiler_params=pltpu.CompilerParams(vmem_limit_bytes=GRANT),
     )(*results)
 
 

time: 38.8 us -> 36.2 us (0.933)
  Pallas kernels: 38 us -> 35.3 us
    pallas_call x1, Pallas kernels: 36.6 us -> 32.8 us  [on_device_quad(): pl.pallas_call(functools.partial(quad_kernel, n), out_shape=tuple((pltpu....]
    pallas_call x1, Pallas kernels: 1.35 us -> 2.51 us  [on_device_quad(): pl.pallas_call(closing_kernel, out_shape=(column, square, column, square,...]
where the time goes in v3:
time: 36.2 us; the launch traced here: 36 us
  Pallas kernels  35.3 us (98%)
  between operations  0.64 us (2%)
    pallas_call x1, Pallas kernels, on_device_quad(): pl.pallas_call(functools.partial(quad_kernel, n), out_shape=tuple((pltpu....  32.8 us
    pallas_call x1, Pallas kernels, on_device_quad(): pl.pallas_call(closing_kernel, out_shape=(column, square, column, square,...  2.51 us

profile of v3, /device:TPU:1, one launch (start us, length us, event | category | flops | bytes accessed | tf_op | source)
XLA Modules:
  0.0 36.0 jit_solution(5545839202368710901)
XLA Ops:
  0.6 32.8 %shard_map.119 = (f32[512,256]{1,0:T(8,128)S(1)}, f32[512,256]{1,0:T(8,128)S(1)}, f32[512,256]{1,0:T(8,128)S(1)}, f32[128,512]{1,0:T(8,128)S(1)}, bf16[2,512,512...) custom-call(f32[8,64,128]{2,1,0:T(8,128)} %known.1, ...), custom_call_target="tpu_custom_call" | custom-call | tf_op jit(solution)/shard_map/pallas_call | solution.py:618
  33.5 2.5 %shard_map.120 = (f32[128,256]{1,0:T(8,128)}, f32[512,256]{1,0:T(8,128)}, f32[128,256]{1,0:T(8,128)}, f32[512,256]{1,0:T(8,128)}, f32[512,256]{1,0:T(8,128)}) custom-call(f32[512,256]{1,0:T(8,128)S(1)} %get-tuple-element.13.diagonal_one, f32[512,256]{1,0:T(8,128)S(1)} %get-tuple-element.14.cross_two, f32[512,256]{1,0:T(8,128)S(1)} %get-tuple-element.15.diagonal_two, ...), custom_call_target="tpu_custom_call" | custom-call | tf_op jit(solution)/shard_map/pallas_call | solution.py:668

commit v4 on v3

--- a/solution.py
+++ b/solution.py
@@ -130,6 +130,7 @@
     corner_two_buf,
     link_split,
     reduced,
+    swelled,
     both,
     k_split,
     local_sem,
@@ -428,12 +429,9 @@
     def block_of(q, i):
         return total[q, k_start + i * part : k_start + (i + 1) * part, :]
 
-    def put_diagonal(col):
-        for q in (2 * col, 2 * col + 1):
+    def put_blocks():
+        for q in (2, 3):
             put(q, q, block_of(q, 0))
-
-    def put_others():
-        for q in (2, 3):
             for i in (1, 2):
                 value = block_of(q, i)
                 put((q + i) % 4, q, value)
@@ -441,7 +439,7 @@
 
     def grow(half):
         rows = slice(half * (one // 2), (half + 1) * (one // 2))
-        reduced[rows, :] = dot3((k_split[0, rows], k_split[1, rows]), (mine_split[0], mine_split[1]))
+        swelled[rows, :] = dot3((k_split[0, rows], k_split[1, rows]), (mine_split[0], mine_split[1]))
 
     def plan(col):
         mine_chunks = common if col == 0 else chunks
@@ -473,9 +471,7 @@
             for k in later[: (len(later) + 1) // 2]:
                 relay(k)
             from_pair(k_start, rows_all)
-            put_diagonal(1)
-            put_others()
-            put_diagonal(0)
+            put_blocks()
             grow(0)
             for k in later[(len(later) + 1) // 2 :]:
                 relay(k)
@@ -490,15 +486,12 @@
             for k in left:
                 if k >= common:
                     relay(k)
-            put_diagonal(1)
-            put_others()
+            put_blocks()
+            grow(0)
+            grow(1)
             from_pair(one, k_start)
             second_half(0, False)
-            from_pair(k_start, k_start + part)
-            put_diagonal(0)
-            grow(0)
-            grow(1)
-            from_pair(k_start + part, k_start + 2 * part)
+            from_pair(k_start, k_start + 2 * part)
 
     for col in range(2):
         pl.when(me_col == col)(functools.partial(plan, col))
@@ -509,13 +502,16 @@
     def mine_at(q):
         return mine_split[0, rows_at(q)], mine_split[1, rows_at(q)]
 
-    lower = split(jnp.concatenate([block_of(0, 1).T, block_of(1, 1)], axis=0))
-    middle = split(jnp.concatenate([block_of(0, 1), block_of(1, 1).T], axis=1))
-    ends = tuple(jnp.concatenate(both_ends, axis=0) for both_ends in zip(mine_at(0), mine_at(2)))
-    outer_term = dot3(lower, mine_at(1))
-    middle_term = dot3(middle, ends)
-    for q, term in ((3, None), (0, outer_term[:part]), (2, outer_term[part:]), (1, middle_term)):
-        value = reduced[rows_at(q), :] if term is None else reduced[rows_at(q), :] + term
+    top = jnp.concatenate([block_of(0, 0), block_of(0, 1).T], axis=1)
+    bottom = jnp.concatenate([block_of(0, 1), block_of(1, 0)], axis=1)
+    two_rows = slice(0, 2 * part)
+    corner = dot3(
+        split(jnp.concatenate([top, bottom], axis=0)), (mine_split[0, two_rows], mine_split[1, two_rows])
+    )
+    below = dot3(split(block_of(1, 1)), mine_at(1))
+    beside = dot3(split(block_of(1, 1).T), mine_at(2))
+    for q, term in ((3, None), (0, corner[:part]), (1, corner[part:] + beside), (2, below)):
+        value = swelled[rows_at(q), :] if term is None else swelled[rows_at(q), :] + term
         grown[0, rows_at(q)], grown[1, rows_at(q)] = split(value)
 
     for i in range(3):
@@ -638,6 +634,7 @@
             pltpu.VMEM((width, hw), f32),
             pltpu.VMEM((2, width, width), bf16),
             pltpu.VMEM((one, width), f32),
+            pltpu.VMEM((one, 2 * hw), f32),
             pltpu.VMEM((2, one, width), bf16),
             pltpu.VMEM((2, one, one), bf16),
             pltpu.SemaphoreType.DMA((8,)),

time: 36.2 us -> 36 us (level)
  no operation moved by 1% of the time
where the time goes in v4:
time: 36 us; the launch traced here: 35.8 us
  Pallas kernels  35.2 us (98%)
  between operations  0.64 us (2%)
    pallas_call x1, Pallas kernels, on_device_quad(): pl.pallas_call(functools.partial(quad_kernel, n), out_shape=tuple((pltpu....  32.7 us
    pallas_call x1, Pallas kernels, on_device_quad(): pl.pallas_call(closing_kernel, out_shape=(column, square, column, square,...  2.51 us

profile of v4, /device:TPU:1, one launch (start us, length us, event | category | flops | bytes accessed | tf_op | source)
XLA Modules:
  0.0 35.8 jit_solution(2458583600590689800)
XLA Ops:
  0.6 32.7 %shard_map.119 = (f32[512,256]{1,0:T(8,128)S(1)}, f32[512,256]{1,0:T(8,128)S(1)}, f32[512,256]{1,0:T(8,128)S(1)}, f32[128,512]{1,0:T(8,128)S(1)}, bf16[2,512,512...) custom-call(f32[8,64,128]{2,1,0:T(8,128)} %known.1, ...), custom_call_target="tpu_custom_call" | custom-call | tf_op jit(solution)/shard_map/pallas_call | solution.py:614
  33.3 2.5 %shard_map.120 = (f32[128,256]{1,0:T(8,128)}, f32[512,256]{1,0:T(8,128)}, f32[128,256]{1,0:T(8,128)}, f32[512,256]{1,0:T(8,128)}, f32[512,256]{1,0:T(8,128)}) custom-call(f32[512,256]{1,0:T(8,128)S(1)} %get-tuple-element.13.diagonal_one, f32[512,256]{1,0:T(8,128)S(1)} %get-tuple-element.14.cross_two, f32[512,256]{1,0:T(8,128)S(1)} %get-tuple-element.15.diagonal_two, ...), custom_call_target="tpu_custom_call" | custom-call | tf_op jit(solution)/shard_map/pallas_call | solution.py:665

commit v5 on v4

--- a/solution.py
+++ b/solution.py
@@ -344,6 +344,7 @@
             held(k, lambda k: cross_copy(k).start())
 
     raw_copy(1, 0).wait_recv()
+    send_raw(1)
     add_pair(0)
 
     @pl.when(inner)
@@ -352,7 +353,6 @@
         raw_copy(2, 0).wait_recv()
         add_quad(0)
 
-    send_raw(1)
     k_copy().wait_recv()
     k_full[...] = k_part[...] + k_peer[...]
     raw[2, my_place] = k_full[:, lanes(my_quarter)]

time: 36 us -> 35.5 us (0.986)
  Pallas kernels: 35.2 us -> 34.7 us
    pallas_call x1, Pallas kernels: 32.7 us -> 32.2 us  [on_device_quad(): pl.pallas_call(functools.partial(quad_kernel, n), out_shape=tuple((pltpu....]
where the time goes in v5:
time: 35.5 us; the launch traced here: 35.3 us
  Pallas kernels  34.7 us (98%)
  between operations  0.64 us (2%)
    pallas_call x1, Pallas kernels, on_device_quad(): pl.pallas_call(functools.partial(quad_kernel, n), out_shape=tuple((pltpu....  32.2 us
    pallas_call x1, Pallas kernels, on_device_quad(): pl.pallas_call(closing_kernel, out_shape=(column, square, column, square,...  2.51 us

profile of v5, /device:TPU:1, one launch (start us, length us, event | category | flops | bytes accessed | tf_op | source)
XLA Modules:
  0.0 35.3 jit_solution(18065698104669001699)
XLA Ops:
  0.6 32.2 %shard_map.119 = (f32[512,256]{1,0:T(8,128)S(1)}, f32[512,256]{1,0:T(8,128)S(1)}, f32[512,256]{1,0:T(8,128)S(1)}, f32[128,512]{1,0:T(8,128)S(1)}, bf16[2,512,512...) custom-call(f32[8,64,128]{2,1,0:T(8,128)} %known.1, ...), custom_call_target="tpu_custom_call" | custom-call | tf_op jit(solution)/shard_map/pallas_call | solution.py:614
  32.8 2.5 %shard_map.120 = (f32[128,256]{1,0:T(8,128)}, f32[512,256]{1,0:T(8,128)}, f32[128,256]{1,0:T(8,128)}, f32[512,256]{1,0:T(8,128)}, f32[512,256]{1,0:T(8,128)}) custom-call(f32[512,256]{1,0:T(8,128)S(1)} %get-tuple-element.13.diagonal_one, f32[512,256]{1,0:T(8,128)S(1)} %get-tuple-element.14.cross_two, f32[512,256]{1,0:T(8,128)S(1)} %get-tuple-element.15.diagonal_two, ...), custom_call_target="tpu_custom_call" | custom-call | tf_op jit(solution)/shard_map/pallas_call | solution.py:665
